TPU v7x, 16 devices: a 4x2x1 block of a 4x4x8 slice. The times are simulated.
16 devices in a mesh: rep: 4 (over y, z, core), pp: 4 (over x).
Axes of the slice: x: 4, y: 2, z: 1, core: 2. Of those that a mesh axis runs over, the one named last changes fastest.
The devices are a block of a 4x4x8 slice.
Arguments:
- x: bfloat16 [32, 512, 512], P('rep'), parts along dimension 0
- dy: bfloat16 [32, 512, 512], P('rep'), parts along dimension 0
- w_gate: bfloat16 [4, 512, 1664], P('pp')
- w_up: bfloat16 [4, 512, 1664], P('pp')
- w_down: bfloat16 [4, 1664, 512], P('pp')
Outputs:
- output 1: bfloat16 [16, 512, 1664], P(('rep', 'pp')), parts along dimension 0
- output 2: bfloat16 [16, 512, 1664], P(('rep', 'pp')), parts along dimension 0
- output 3: bfloat16 [16, 1664, 512], P(('rep', 'pp')), parts along dimension 0
There are 4 independent parts. A program takes and returns all parts, laid end to end along the dimension named above; an argument that names none is the same for every part.
All inputs are finite; a program needn't handle non-finite values.
Results may differ from a plain program's by a relative error of at most 0.018.
Values are sent between devices in bfloat16 or wider.
A program may use at most 768 MiB of HBM per device.

v0:
```python
import functools

import jax
import jax.numpy as jnp
from jax import lax
from jax.experimental import pallas as pl
from jax.experimental.pallas import tpu as pltpu
from jax.sharding import PartitionSpec as P

CHUNK = 128
BLOCK = 256
HALF = BLOCK // 2
OFF = 5
EPS = 1e-6
F32, BF16 = jnp.float32, jnp.bfloat16
MESH = pl.DeviceIdType.MESH


def dot(a, b):
    return jnp.dot(a, b, preferred_element_type=F32)


def sigmoid(x):
    return 0.5 * jnp.tanh(0.5 * x) + 0.5


def kernel(
    stages, per, chunks,
    x_ref, dy_ref, wg_ref, wu_ref, wd_ref,
    og_ref, ou_ref, od_ref,
    kept, byin, out, wgu, wgut, wd, wdt, rhs, lhs, total, midc, dguc,
    fsend, frecv, bsend, brecv, wsem, osem,
):
    me = lax.axis_index("pp")
    behind = stages - 1 - me
    first, last = me == 0, behind == 0
    right, left = lax.rem(me + 1, stages), lax.rem(me + stages - 1, stages)
    d, ff = wg_ref.shape
    nb = ff // HALF
    nd = pl.cdiv(ff, BLOCK)
    quarter = (nb + nd) // per

    loads = [pltpu.make_async_copy(wd_ref, wd, wsem.at[0])]
    for j in range(nb):
        cols = pl.ds(j * HALF, HALF)
        loads.append(pltpu.make_async_copy(wg_ref.at[:, cols], wgu.at[j, :, pl.ds(0, HALF)], wsem.at[1 + 2 * j]))
        loads.append(pltpu.make_async_copy(wu_ref.at[:, cols], wgu.at[j, :, pl.ds(HALF, HALF)], wsem.at[2 + 2 * j]))
    for load in loads:
        load.start()

    def x_load(k):
        return pltpu.make_async_copy(x_ref.at[k], kept.at[k], frecv.at[k])

    def dy_load(k):
        return pltpu.make_async_copy(dy_ref.at[k], byin.at[k], brecv.at[k])

    @pl.when(first)
    def _():
        def go(k, c):
            x_load(k).start()
            return c

        lax.fori_loop(0, chunks, go, 0)

    @pl.when(last)
    def _():
        def go(k, c):
            dy_load(k).start()
            return c

        lax.fori_loop(0, chunks, go, 0)

    barrier = pltpu.get_barrier_semaphore()
    for side in (left, right):
        pl.semaphore_signal(barrier, inc=1, device_id={"pp": side}, device_id_type=MESH)

    total[...] = jnp.zeros_like(total)
    rhs[:, nb + nd - 1] = jnp.zeros_like(rhs[:, nb + nd - 1])
    wdt[nd - 1] = jnp.zeros_like(wdt[nd - 1])
    for load in loads:
        load.wait()
    pl.semaphore_wait(barrier, 2)

    def f_copy(k):
        return pltpu.make_async_remote_copy(
            src_ref=out.at[k], dst_ref=kept.at[k], send_sem=fsend.at[k], recv_sem=frecv.at[k],
            device_id={"pp": right}, device_id_type=MESH,
        )

    def b_copy(k):
        return pltpu.make_async_remote_copy(
            src_ref=out.at[k], dst_ref=byin.at[k], send_sem=bsend.at[k], recv_sem=brecv.at[k],
            device_id={"pp": left}, device_id_type=MESH,
        )

    def normed(h):
        wide = h.astype(F32)
        scale = lax.rsqrt(jnp.mean(wide * wide, -1, keepdims=True) + EPS)
        return wide, scale, (wide * scale).astype(BF16)

    def forward(k):
        x_load(k).wait()
        wide, _, a = normed(kept[k])
        for j in range(nb):
            gu = dot(a, wgu[j])
            g, u = gu[:, :HALF], gu[:, HALF:]
            midc[:, j * HALF : (j + 1) * HALF] = (g * sigmoid(g) * u).astype(BF16)
        y = dot(midc[...], wd[...]).astype(BF16)
        out[k] = (wide + y.astype(F32)).astype(BF16)
        f_copy(k).start()

    def backward(k):
        slot = lax.rem(lax.div(k, per), 2)
        rows = pl.ds(pl.multiple_of(lax.rem(k, per) * CHUNK, CHUNK), CHUNK)

        @pl.when(last)
        def _():
            x_load(k).wait()

        dy_load(k).wait()

        @pl.when(jnp.logical_not(last))
        def _():
            f_copy(k).wait_send()

        by = byin[k]
        wide, scale, a = normed(kept[k])
        lhs[slot, 0, :, rows] = a.astype(F32).T.astype(BF16)
        lhs[slot, 1, :, rows] = by.astype(F32).T.astype(BF16)
        for jj in range(nd):
            dmid2 = dot(by, wdt[jj]).astype(BF16).astype(F32)
            for part in range(2):
                j = 2 * jj + part
                if j >= nb:
                    break
                dmid = dmid2[:, part * HALF : (part + 1) * HALF]
                gu = dot(a, wgu[j])
                g, u = gu[:, :HALF], gu[:, HALF:]
                s = sigmoid(g)
                silu = g * s
                dup = (dmid * silu).astype(BF16)
                dgate = (dmid * u * (s + silu * (1.0 - s))).astype(BF16)
                rhs[slot, nb + jj, rows, part * HALF : (part + 1) * HALF] = (silu * u).astype(BF16)
                rhs[slot, j, rows, :HALF] = dgate
                rhs[slot, j, rows, HALF:] = dup
                dguc[:, j * BLOCK : j * BLOCK + HALF] = dgate
                dguc[:, j * BLOCK + HALF : (j + 1) * BLOCK] = dup

        @pl.when(jnp.logical_not(first))
        def _():
            wide, scale, _ = normed(kept[k])
            da = dot(dguc[...], wgut[...]).astype(BF16).astype(F32)
            lean = jnp.mean(da * wide, -1, keepdims=True) * scale * scale * scale
            dh = (da * scale - wide * lean).astype(BF16)
            out[k] = (byin[k].astype(F32) + dh.astype(F32)).astype(BF16)
            b_copy(k).start()

    def products(k):
        slot = lax.rem(lax.div(k, per), 2)
        start = lax.rem(k, per) * quarter
        for i in range(quarter):
            q = start + i
            which = jnp.where(q >= nb, 1, 0)
            term = dot(lhs[slot, which], rhs[slot, q]).astype(BF16)
            total[q] += term.astype(F32)

    def transposed():
        for j in range(nb):
            wgut[j * BLOCK : (j + 1) * BLOCK, :] = wgu[j].astype(F32).T.astype(BF16)
        for jj in range(nd):
            lo, hi = jj * BLOCK, min(ff, (jj + 1) * BLOCK)
            wdt[jj, :, : hi - lo] = wd[lo:hi, :].astype(F32).T.astype(BF16)

    def step(i, carry):
        f, b = i, i - OFF * behind
        w = b - per

        @pl.when((f < chunks) & jnp.logical_not(last))
        def _():
            forward(f)

        @pl.when(i == jnp.where(first, 3, 0))
        def _():
            transposed()

        @pl.when((b >= 0) & (b < chunks))
        def _():
            backward(b)

        @pl.when((w >= 0) & (w < chunks))
        def _():
            products(w)

        return carry

    lax.fori_loop(0, chunks + OFF * (stages - 1) + per, step, 0)

    stores = []
    for jj in range(nd):
        lo, hi = jj * BLOCK, min(ff, (jj + 1) * BLOCK)
        wd[lo:hi, :] = total[nb + jj].T[: hi - lo].astype(BF16)
    stores.append(pltpu.make_async_copy(wd, od_ref, osem.at[0]))
    stores[-1].start()
    for j in range(nb):
        cols = pl.ds(j * HALF, HALF)
        rhs[0, j] = total[j].astype(BF16)
        stores.append(pltpu.make_async_copy(rhs.at[0, j, :, pl.ds(0, HALF)], og_ref.at[:, cols], osem.at[1 + 2 * j]))
        stores[-1].start()
        stores.append(pltpu.make_async_copy(rhs.at[0, j, :, pl.ds(HALF, HALF)], ou_ref.at[:, cols], osem.at[2 + 2 * j]))
        stores[-1].start()
    for store in stores:
        store.wait()

    @pl.when(jnp.logical_not(first))
    def _():
        def sent(k, c):
            b_copy(k).wait_send()
            return c

        lax.fori_loop(0, chunks, sent, 0)


def solution(mesh):
    stages = mesh.shape["pp"]

    def step(x, dy, w_gate, w_up, w_down):
        micro, tokens, d = x.shape
        ff = w_gate.shape[-1]
        per = tokens // CHUNK
        chunks = micro * per
        nb, nd = ff // HALF, pl.cdiv(ff, BLOCK)
        flat = (chunks, CHUNK, d)
        grads = pl.pallas_call(
            functools.partial(kernel, stages, per, chunks),
            out_shape=[
                jax.ShapeDtypeStruct((d, ff), BF16),
                jax.ShapeDtypeStruct((d, ff), BF16),
                jax.ShapeDtypeStruct((ff, d), BF16),
            ],
            in_specs=[pl.BlockSpec(memory_space=pl.ANY)] * 5,
            out_specs=[pl.BlockSpec(memory_space=pl.ANY)] * 3,
            scratch_shapes=[
                pltpu.VMEM(flat, BF16),
                pltpu.VMEM(flat, BF16),
                pltpu.VMEM(flat, BF16),
                pltpu.VMEM((nb, d, BLOCK), BF16),
                pltpu.VMEM((nb * BLOCK, d), BF16),
                pltpu.VMEM((ff, d), BF16),
                pltpu.VMEM((nd, d, BLOCK), BF16),
                pltpu.VMEM((2, nb + nd, tokens, BLOCK), BF16),
                pltpu.VMEM((2, 2, d, tokens), BF16),
                pltpu.VMEM((nb + nd, d, BLOCK), F32),
                pltpu.VMEM((CHUNK, ff), BF16),
                pltpu.VMEM((CHUNK, nb * BLOCK), BF16),
                pltpu.SemaphoreType.DMA((chunks,)),
                pltpu.SemaphoreType.DMA((chunks,)),
                pltpu.SemaphoreType.DMA((chunks,)),
                pltpu.SemaphoreType.DMA((chunks,)),
                pltpu.SemaphoreType.DMA((1 + 2 * nb,)),
                pltpu.SemaphoreType.DMA((1 + 2 * nb,)),
            ],
            compiler_params=pltpu.CompilerParams(
                collective_id=0, has_side_effects=True, vmem_limit_bytes=67_000_000
            ),
        )(x.reshape(flat), dy.reshape(flat), w_gate[0], w_up[0], w_down[0])
        return tuple(g[None] for g in grads)

    return jax.shard_map(
        step,
        mesh=mesh,
        in_specs=(P("rep", None, None),) * 2 + (P("pp", None, None),) * 3,
        out_specs=(P(("rep", "pp"), None, None),) * 3,
        check_vma=False,
    )
```

profile of v0, /device:TPU:112, one launch (start us, length us, event | category | flops | bytes accessed | tf_op | source)
XLA Modules:
  0.0 162.6 jit_solution(16876937481911505907)
XLA Ops:
  0.6 155.8 %shard_map.76 = (bf16[512,1664]{1,0:T(8,128)(2,1)}, bf16[512,1664]{1,0:T(8,128)(2,1)}, bf16[1664,512]{1,0:T(8,128)(2,1)}) custom-call(bf16[32,128,512]{2,1,0:T(8,128)(2,1)} %bitcast.8, bf16[32,128,512]{2,1,0:T(8,128)(2,1)} %bitcast.9, bf16[512,1664]{1,0:T(8,128)(2,1)} %bitcast.10, bf16[512,1664]{1,0:T(8,128)(2,1)} %bitcast.11, bf16[1664,512]{1,0:T(8,128)(2,1)} %bitcast.12), custom_call_target="tpu_custom_call" | custom-call | tf_op jit(solution)/shard_map/pallas_call | solution.py:233
  156.5 0.0 copy-start.1
  156.5 2.9 %copy.11 = bf16[1,512,1664]{2,1,0:T(8,128)(2,1)} copy(bf16[1,512,1664]{2,1,0:T(8,128)(2,1)} %bitcast.15) | data formatting | bytes 3407872
  159.4 0.0 copy-done.1
  159.4 0.0 copy-start
  159.4 1.2 copy.12
  160.6 0.9 copy-done
  161.4 1.2 copy.13
Async XLA Ops:
  156.5 2.9 %copy-start.1 = (bf16[512,1664]{1,0:T(8,128)(2,1)S(1)}, bf16[512,1664]{1,0:T(8,128)(2,1)}, u32[]{:S(2)}) copy-start(bf16[512,1664]{1,0:T(8,128)(2,1)} %get-tuple-element.7) | copy-start | bytes 5111812
  159.4 2.1 %copy-start = (bf16[1664,512]{1,0:T(8,128)(2,1)S(1)}, bf16[1664,512]{1,0:T(8,128)(2,1)}, u32[]{:S(2)}) copy-start(bf16[1664,512]{1,0:T(8,128)(2,1)} %get-tuple-element.8) | copy-start | bytes 5111812
where the time goes:
time: 163 us
  Pallas kernels  156 us (96%)
  local copies, waits for them, and re-layouts  6.15 us (4%)
    pallas_call x1, Pallas kernels, step(): pl.pallas_call(functools.partial(kernel, stages, per, chunks), out_shape=...  156 us
    unnamed x7, local copies, waits for them, and re-layouts  6.15 us

commit v1 on v0

--- a/solution.py
+++ b/solution.py
@@ -11,6 +11,8 @@
 BLOCK = 256
 HALF = BLOCK // 2
 OFF = 5
+AHEAD = 5
+OUT = 4
 EPS = 1e-6
 F32, BF16 = jnp.float32, jnp.bfloat16
 MESH = pl.DeviceIdType.MESH
@@ -28,7 +30,7 @@
     stages, per, chunks,
     x_ref, dy_ref, wg_ref, wu_ref, wd_ref,
     og_ref, ou_ref, od_ref,
-    kept, byin, out, wgu, wgut, wd, wdt, rhs, lhs, total, midc, dguc,
+    kept, byin, fout, bout, wgu, wgut, wd, wdt, rhs, lhs, total, mids, slopes, dguc,
     fsend, frecv, bsend, brecv, wsem, osem,
 ):
     me = lax.axis_index("pp")
@@ -48,11 +50,15 @@
     for load in loads:
         load.start()
 
+    reach = OFF * (stages - 1)
+    n_kept, n_by, n_mid = kept.shape[0], byin.shape[0], mids.shape[0]
+    assert n_kept > reach and n_by > reach and n_mid > OFF * (stages - 2)
+
     def x_load(k):
-        return pltpu.make_async_copy(x_ref.at[k], kept.at[k], frecv.at[k])
+        return pltpu.make_async_copy(x_ref.at[k], kept.at[lax.rem(k, n_kept)], frecv.at[k])
 
     def dy_load(k):
-        return pltpu.make_async_copy(dy_ref.at[k], byin.at[k], brecv.at[k])
+        return pltpu.make_async_copy(dy_ref.at[k], byin.at[lax.rem(k, n_by)], brecv.at[k])
 
     @pl.when(first)
     def _():
@@ -60,7 +66,7 @@
             x_load(k).start()
             return c
 
-        lax.fori_loop(0, chunks, go, 0)
+        lax.fori_loop(0, min(chunks, n_kept), go, 0)
 
     @pl.when(last)
     def _():
@@ -68,7 +74,7 @@
             dy_load(k).start()
             return c
 
-        lax.fori_loop(0, chunks, go, 0)
+        lax.fori_loop(0, min(chunks, n_by), go, 0)
 
     barrier = pltpu.get_barrier_semaphore()
     for side in (left, right):
@@ -83,13 +89,13 @@
 
     def f_copy(k):
         return pltpu.make_async_remote_copy(
-            src_ref=out.at[k], dst_ref=kept.at[k], send_sem=fsend.at[k], recv_sem=frecv.at[k],
+            src_ref=fout.at[lax.rem(k, OUT)], dst_ref=kept.at[lax.rem(k, n_kept)], send_sem=fsend.at[k], recv_sem=frecv.at[k],
             device_id={"pp": right}, device_id_type=MESH,
         )
 
     def b_copy(k):
         return pltpu.make_async_remote_copy(
-            src_ref=out.at[k], dst_ref=byin.at[k], send_sem=bsend.at[k], recv_sem=brecv.at[k],
+            src_ref=bout.at[lax.rem(k, OUT)], dst_ref=byin.at[lax.rem(k, n_by)], send_sem=bsend.at[k], recv_sem=brecv.at[k],
             device_id={"pp": left}, device_id_type=MESH,
         )
 
@@ -100,17 +106,29 @@
 
     def forward(k):
         x_load(k).wait()
-        wide, _, a = normed(kept[k])
+        slot = lax.rem(k, n_mid)
+        wide, _, a = normed(kept[lax.rem(k, n_kept)])
         for j in range(nb):
             gu = dot(a, wgu[j])
             g, u = gu[:, :HALF], gu[:, HALF:]
-            midc[:, j * HALF : (j + 1) * HALF] = (g * sigmoid(g) * u).astype(BF16)
-        y = dot(midc[...], wd[...]).astype(BF16)
-        out[k] = (wide + y.astype(F32)).astype(BF16)
+            s = sigmoid(g)
+            silu = g * s
+            mids[slot, :, j * HALF : (j + 1) * HALF] = (silu * u).astype(BF16)
+            slopes[slot, j, :, :HALF] = u * (s + silu * (1.0 - s))
+            slopes[slot, j, :, HALF:] = silu
+        y = dot(mids[slot], wd[...]).astype(BF16)
+
+        @pl.when(k >= OUT)
+        def _():
+            f_copy(k - OUT).wait_send()
+
+        fout[lax.rem(k, OUT)] = (wide + y.astype(F32)).astype(BF16)
         f_copy(k).start()
 
     def backward(k):
         slot = lax.rem(lax.div(k, per), 2)
+        mine = lax.rem(k, n_mid)
+        here = lax.rem(k, n_kept)
         rows = pl.ds(pl.multiple_of(lax.rem(k, per) * CHUNK, CHUNK), CHUNK)
 
         @pl.when(last)
@@ -119,41 +137,66 @@
 
         dy_load(k).wait()
 
-        @pl.when(jnp.logical_not(last))
-        def _():
-            f_copy(k).wait_send()
-
-        by = byin[k]
-        wide, scale, a = normed(kept[k])
-        lhs[slot, 0, :, rows] = a.astype(F32).T.astype(BF16)
-        lhs[slot, 1, :, rows] = by.astype(F32).T.astype(BF16)
-        for jj in range(nd):
-            dmid2 = dot(by, wdt[jj]).astype(BF16).astype(F32)
-            for part in range(2):
-                j = 2 * jj + part
-                if j >= nb:
-                    break
-                dmid = dmid2[:, part * HALF : (part + 1) * HALF]
+        def share(j, dmid, slope, silu, mid):
+            jj, part = j // 2, j % 2
+            dgate, dup = (dmid * slope).astype(BF16), (dmid * silu).astype(BF16)
+            rhs[slot, nb + jj, rows, part * HALF : (part + 1) * HALF] = mid
+            rhs[slot, j, rows, :HALF] = dgate
+            rhs[slot, j, rows, HALF:] = dup
+            dguc[:, j * BLOCK : j * BLOCK + HALF] = dgate
+            dguc[:, j * BLOCK + HALF : (j + 1) * BLOCK] = dup
+
+        def by_mid(by):
+            for jj in range(nd):
+                two = dot(by, wdt[jj]).astype(BF16).astype(F32)
+                for part in range(min(2, nb - 2 * jj)):
+                    yield 2 * jj + part, two[:, part * HALF : (part + 1) * HALF]
+
+        def turned(a, by):
+            lhs[slot, 0, :, rows] = a.astype(F32).T.astype(BF16)
+            lhs[slot, 1, :, rows] = by.astype(F32).T.astype(BF16)
+
+        @pl.when(first | last)
+        def _():
+            by = byin[lax.rem(k, n_by)]
+            _, _, a = normed(kept[here])
+            turned(a, by)
+            for j, dmid in by_mid(by):
                 gu = dot(a, wgu[j])
                 g, u = gu[:, :HALF], gu[:, HALF:]
                 s = sigmoid(g)
                 silu = g * s
-                dup = (dmid * silu).astype(BF16)
-                dgate = (dmid * u * (s + silu * (1.0 - s))).astype(BF16)
-                rhs[slot, nb + jj, rows, part * HALF : (part + 1) * HALF] = (silu * u).astype(BF16)
-                rhs[slot, j, rows, :HALF] = dgate
-                rhs[slot, j, rows, HALF:] = dup
-                dguc[:, j * BLOCK : j * BLOCK + HALF] = dgate
-                dguc[:, j * BLOCK + HALF : (j + 1) * BLOCK] = dup
+                share(j, dmid, u * (s + silu * (1.0 - s)), silu, (silu * u).astype(BF16))
+
+        @pl.when(jnp.logical_not(first | last))
+        def _():
+            by = byin[lax.rem(k, n_by)]
+            _, _, a = normed(kept[here])
+            turned(a, by)
+            for j, dmid in by_mid(by):
+                share(j, dmid, slopes[mine, j, :, :HALF], slopes[mine, j, :, HALF:], mids[mine, :, j * HALF : (j + 1) * HALF])
 
         @pl.when(jnp.logical_not(first))
         def _():
-            wide, scale, _ = normed(kept[k])
+            wide, scale, _ = normed(kept[here])
             da = dot(dguc[...], wgut[...]).astype(BF16).astype(F32)
             lean = jnp.mean(da * wide, -1, keepdims=True) * scale * scale * scale
             dh = (da * scale - wide * lean).astype(BF16)
-            out[k] = (byin[k].astype(F32) + dh.astype(F32)).astype(BF16)
+
+            @pl.when(k >= OUT)
+            def _():
+                b_copy(k - OUT).wait_send()
+
+            bout[lax.rem(k, OUT)] = (byin[lax.rem(k, n_by)].astype(F32) + dh.astype(F32)).astype(BF16)
             b_copy(k).start()
+
+        @pl.when(first & (k + n_kept < chunks))
+        def _():
+            x_load(k + n_kept).start()
+
+        @pl.when(last & (k + n_by < chunks))
+        def _():
+            dy_load(k + n_by).start()
 
     def products(k):
         slot = lax.rem(lax.div(k, per), 2)
@@ -175,13 +218,13 @@
         f, b = i, i - OFF * behind
         w = b - per
 
+        @pl.when(i == jnp.where(first, 3, 0))
+        def _():
+            transposed()
+
         @pl.when((f < chunks) & jnp.logical_not(last))
         def _():
             forward(f)
-
-        @pl.when(i == jnp.where(first, 3, 0))
-        def _():
-            transposed()
 
         @pl.when((b >= 0) & (b < chunks))
         def _():
@@ -211,13 +254,20 @@
     for store in stores:
         store.wait()
 
+    def sent(copy):
+        def one(k, c):
+            copy(k).wait_send()
+            return c
+
+        lax.fori_loop(max(0, chunks - OUT), chunks, one, 0)
+
+    @pl.when(jnp.logical_not(last))
+    def _():
+        sent(f_copy)
+
     @pl.when(jnp.logical_not(first))
     def _():
-        def sent(k, c):
-            b_copy(k).wait_send()
-            return c
-
-        lax.fori_loop(0, chunks, sent, 0)
+        sent(b_copy)
 
 
 def solution(mesh):
@@ -230,6 +280,7 @@
         chunks = micro * per
         nb, nd = ff // HALF, pl.cdiv(ff, BLOCK)
         flat = (chunks, CHUNK, d)
+        reach, saved = OFF * (stages - 1), OFF * (stages - 2) + 1
         grads = pl.pallas_call(
             functools.partial(kernel, stages, per, chunks),
             out_shape=[
@@ -240,9 +291,10 @@
             in_specs=[pl.BlockSpec(memory_space=pl.ANY)] * 5,
             out_specs=[pl.BlockSpec(memory_space=pl.ANY)] * 3,
             scratch_shapes=[
-                pltpu.VMEM(flat, BF16),
-                pltpu.VMEM(flat, BF16),
-                pltpu.VMEM(flat, BF16),
+                pltpu.VMEM((reach + AHEAD, CHUNK, d), BF16),
+                pltpu.VMEM((reach + 1, CHUNK, d), BF16),
+                pltpu.VMEM((OUT, CHUNK, d), BF16),
+                pltpu.VMEM((OUT, CHUNK, d), BF16),
                 pltpu.VMEM((nb, d, BLOCK), BF16),
                 pltpu.VMEM((nb * BLOCK, d), BF16),
                 pltpu.VMEM((ff, d), BF16),
@@ -250,7 +302,8 @@
                 pltpu.VMEM((2, nb + nd, tokens, BLOCK), BF16),
                 pltpu.VMEM((2, 2, d, tokens), BF16),
                 pltpu.VMEM((nb + nd, d, BLOCK), F32),
-                pltpu.VMEM((CHUNK, ff), BF16),
+                pltpu.VMEM((saved, CHUNK, ff), BF16),
+                pltpu.VMEM((saved, nb, CHUNK, BLOCK), F32),
                 pltpu.VMEM((CHUNK, nb * BLOCK), BF16),
                 pltpu.SemaphoreType.DMA((chunks,)),
                 pltpu.SemaphoreType.DMA((chunks,)),

time: 163 us -> 154 us (0.945)
  Pallas kernels: 156 us -> 147 us
    pallas_call x1, Pallas kernels: 156 us -> 147 us  [step(): pl.pallas_call(functools.partial(kernel, stages, per, chunks), out_shape=...]
where the time goes in v1:
time: 154 us
  Pallas kernels  147 us (95%)
  local copies, waits for them, and re-layouts  6.15 us (4%)
    pallas_call x1, Pallas kernels, step(): pl.pallas_call(functools.partial(kernel, stages, per, chunks), out_shape=...  147 us
    unnamed x7, local copies, waits for them, and re-layouts  6.15 us

profile of v1, /device:TPU:112, one launch (start us, length us, event | category | flops | bytes accessed | tf_op | source)
XLA Modules:
  0.0 154.2 jit_solution(5670616887143542544)
XLA Ops:
  0.6 147.4 %shard_map.76 = (bf16[512,1664]{1,0:T(8,128)(2,1)}, bf16[512,1664]{1,0:T(8,128)(2,1)}, bf16[1664,512]{1,0:T(8,128)(2,1)}) custom-call(bf16[32,128,512]{2,1,0:T(8,128)(2,1)} %bitcast.8, bf16[32,128,512]{2,1,0:T(8,128)(2,1)} %bitcast.9, bf16[512,1664]{1,0:T(8,128)(2,1)} %bitcast.10, bf16[512,1664]{1,0:T(8,128)(2,1)} %bitcast.11, bf16[1664,512]{1,0:T(8,128)(2,1)} %bitcast.12), custom_call_target="tpu_custom_call" | custom-call | tf_op jit(solution)/shard_map/pallas_call | solution.py:284
  148.1 0.0 copy-start.1
  148.1 2.9 %copy.11 = bf16[1,512,1664]{2,1,0:T(8,128)(2,1)} copy(bf16[1,512,1664]{2,1,0:T(8,128)(2,1)} %bitcast.15) | data formatting | bytes 3407872
  151.0 0.0 copy-done.1
  151.0 0.0 copy-start
  151.0 1.2 copy.12
  152.2 0.9 copy-done
  153.0 1.2 copy.13
Async XLA Ops:
  148.1 2.9 %copy-start.1 = (bf16[512,1664]{1,0:T(8,128)(2,1)S(1)}, bf16[512,1664]{1,0:T(8,128)(2,1)}, u32[]{:S(2)}) copy-start(bf16[512,1664]{1,0:T(8,128)(2,1)} %get-tuple-element.7) | copy-start | bytes 5111812
  151.0 2.1 %copy-start = (bf16[1664,512]{1,0:T(8,128)(2,1)S(1)}, bf16[1664,512]{1,0:T(8,128)(2,1)}, u32[]{:S(2)}) copy-start(bf16[1664,512]{1,0:T(8,128)(2,1)} %get-tuple-element.8) | copy-start | bytes 5111812

commit v2 on v1

--- a/solution.py
+++ b/solution.py
@@ -12,6 +12,7 @@
 HALF = BLOCK // 2
 OFF = 5
 AHEAD = 5
+STRIP = 32
 OUT = 4
 EPS = 1e-6
 F32, BF16 = jnp.float32, jnp.bfloat16
@@ -30,8 +31,8 @@
     stages, per, chunks,
     x_ref, dy_ref, wg_ref, wu_ref, wd_ref,
     og_ref, ou_ref, od_ref,
-    kept, byin, fout, bout, wgu, wgut, wd, wdt, rhs, lhs, total, mids, slopes, dguc,
-    fsend, frecv, bsend, brecv, wsem, osem,
+    kept, byin, fout, bout, wgu, wgut, wd, wdt, rhs, lhs, total, mids, slopes,
+    fsend, frecv, bsend, brecv, wsem,
 ):
     me = lax.axis_index("pp")
     behind = stages - 1 - me
@@ -52,7 +53,7 @@
 
     reach = OFF * (stages - 1)
     n_kept, n_by, n_mid = kept.shape[0], byin.shape[0], mids.shape[0]
-    assert n_kept > reach and n_by > reach and n_mid > OFF * (stages - 2)
+    assert n_kept > reach and n_by > reach and n_mid >= OFF * (stages - 2)
 
     def x_load(k):
         return pltpu.make_async_copy(x_ref.at[k], kept.at[lax.rem(k, n_kept)], frecv.at[k])
@@ -106,6 +107,11 @@
 
     def forward(k):
         x_load(k).wait()
+
+        @pl.when(k >= OUT)
+        def _():
+            f_copy(k - OUT).wait_send()
+
         slot = lax.rem(k, n_mid)
         wide, _, a = normed(kept[lax.rem(k, n_kept)])
         for j in range(nb):
@@ -117,11 +123,6 @@
             slopes[slot, j, :, :HALF] = u * (s + silu * (1.0 - s))
             slopes[slot, j, :, HALF:] = silu
         y = dot(mids[slot], wd[...]).astype(BF16)
-
-        @pl.when(k >= OUT)
-        def _():
-            f_copy(k - OUT).wait_send()
-
         fout[lax.rem(k, OUT)] = (wide + y.astype(F32)).astype(BF16)
         f_copy(k).start()
 
@@ -135,60 +136,57 @@
         def _():
             x_load(k).wait()
 
+        @pl.when(jnp.logical_not(first) & (k >= OUT))
+        def _():
+            b_copy(k - OUT).wait_send()
+
         dy_load(k).wait()
 
-        def share(j, dmid, slope, silu, mid):
-            jj, part = j // 2, j % 2
-            dgate, dup = (dmid * slope).astype(BF16), (dmid * silu).astype(BF16)
-            rhs[slot, nb + jj, rows, part * HALF : (part + 1) * HALF] = mid
-            rhs[slot, j, rows, :HALF] = dgate
-            rhs[slot, j, rows, HALF:] = dup
-            dguc[:, j * BLOCK : j * BLOCK + HALF] = dgate
-            dguc[:, j * BLOCK + HALF : (j + 1) * BLOCK] = dup
-
-        def by_mid(by):
+        def chunk(again, onward):
+            by = byin[lax.rem(k, n_by)]
+            _, scale, a = normed(kept[here])
+            lhs[slot, 0, :, rows] = a.astype(F32).T.astype(BF16)
+            lhs[slot, 1, :, rows] = by.astype(F32).T.astype(BF16)
             for jj in range(nd):
                 two = dot(by, wdt[jj]).astype(BF16).astype(F32)
                 for part in range(min(2, nb - 2 * jj)):
-                    yield 2 * jj + part, two[:, part * HALF : (part + 1) * HALF]
-
-        def turned(a, by):
-            lhs[slot, 0, :, rows] = a.astype(F32).T.astype(BF16)
-            lhs[slot, 1, :, rows] = by.astype(F32).T.astype(BF16)
-
-        @pl.when(first | last)
-        def _():
-            by = byin[lax.rem(k, n_by)]
-            _, _, a = normed(kept[here])
-            turned(a, by)
-            for j, dmid in by_mid(by):
-                gu = dot(a, wgu[j])
-                g, u = gu[:, :HALF], gu[:, HALF:]
-                s = sigmoid(g)
-                silu = g * s
-                share(j, dmid, u * (s + silu * (1.0 - s)), silu, (silu * u).astype(BF16))
+                    j = 2 * jj + part
+                    dmid = two[:, part * HALF : (part + 1) * HALF]
+                    if again:
+                        gu = dot(a, wgu[j])
+                        g, u = gu[:, :HALF], gu[:, HALF:]
+                        s = sigmoid(g)
+                        silu = g * s
+                        slope, mid = u * (s + silu * (1.0 - s)), (silu * u).astype(BF16)
+                    else:
+                        slope, silu = slopes[mine, j, :, :HALF], slopes[mine, j, :, HALF:]
+                        mid = mids[mine, :, j * HALF : (j + 1) * HALF]
+                    dgate, dup = (dmid * slope).astype(BF16), (dmid * silu).astype(BF16)
+                    rhs[slot, nb + jj, rows, part * HALF : (part + 1) * HALF] = mid
+                    rhs[slot, j, rows, :HALF] = dgate
+                    rhs[slot, j, rows, HALF:] = dup
+            if onward:
+                da = dot(jnp.concatenate([rhs[slot, j, rows] for j in range(nb)], axis=1), wgut[...])
+                for lo in range(0, CHUNK, STRIP):
+                    part = slice(lo, lo + STRIP)
+                    wide, given = kept[here, part].astype(F32), byin[lax.rem(k, n_by), part].astype(F32)
+                    lead, each = scale[part], da[part].astype(BF16).astype(F32)
+                    lean = jnp.mean(each * wide, -1, keepdims=True) * lead * lead * lead
+                    dh = (each * lead - wide * lean).astype(BF16)
+                    bout[lax.rem(k, OUT), part] = (given + dh.astype(F32)).astype(BF16)
+                b_copy(k).start()
+
+        @pl.when(first)
+        def _():
+            chunk(True, False)
+
+        @pl.when(last)
+        def _():
+            chunk(True, True)
 
         @pl.when(jnp.logical_not(first | last))
         def _():
-            by = byin[lax.rem(k, n_by)]
-            _, _, a = normed(kept[here])
-            turned(a, by)
-            for j, dmid in by_mid(by):
-                share(j, dmid, slopes[mine, j, :, :HALF], slopes[mine, j, :, HALF:], mids[mine, :, j * HALF : (j + 1) * HALF])
-
-        @pl.when(jnp.logical_not(first))
-        def _():
-            wide, scale, _ = normed(kept[here])
-            da = dot(dguc[...], wgut[...]).astype(BF16).astype(F32)
-            lean = jnp.mean(da * wide, -1, keepdims=True) * scale * scale * scale
-            dh = (da * scale - wide * lean).astype(BF16)
-
-            @pl.when(k >= OUT)
-            def _():
-                b_copy(k - OUT).wait_send()
-
-            bout[lax.rem(k, OUT)] = (byin[lax.rem(k, n_by)].astype(F32) + dh.astype(F32)).astype(BF16)
-            b_copy(k).start()
+            chunk(False, True)
 
         @pl.when(first & (k + n_kept < chunks))
         def _():
@@ -222,14 +220,14 @@
         def _():
             transposed()
 
+        @pl.when((b >= 0) & (b < chunks))
+        def _():
+            backward(b)
+
         @pl.when((f < chunks) & jnp.logical_not(last))
         def _():
             forward(f)
 
-        @pl.when((b >= 0) & (b < chunks))
-        def _():
-            backward(b)
-
         @pl.when((w >= 0) & (w < chunks))
         def _():
             products(w)
@@ -238,21 +236,13 @@
 
     lax.fori_loop(0, chunks + OFF * (stages - 1) + per, step, 0)
 
-    stores = []
     for jj in range(nd):
         lo, hi = jj * BLOCK, min(ff, (jj + 1) * BLOCK)
-        wd[lo:hi, :] = total[nb + jj].T[: hi - lo].astype(BF16)
-    stores.append(pltpu.make_async_copy(wd, od_ref, osem.at[0]))
-    stores[-1].start()
+        od_ref[lo:hi, :] = total[nb + jj].T[: hi - lo].astype(BF16)
     for j in range(nb):
-        cols = pl.ds(j * HALF, HALF)
-        rhs[0, j] = total[j].astype(BF16)
-        stores.append(pltpu.make_async_copy(rhs.at[0, j, :, pl.ds(0, HALF)], og_ref.at[:, cols], osem.at[1 + 2 * j]))
-        stores[-1].start()
-        stores.append(pltpu.make_async_copy(rhs.at[0, j, :, pl.ds(HALF, HALF)], ou_ref.at[:, cols], osem.at[2 + 2 * j]))
-        stores[-1].start()
-    for store in stores:
-        store.wait()
+        cols = slice(j * HALF, (j + 1) * HALF)
+        og_ref[:, cols] = total[j, :, :HALF].astype(BF16)
+        ou_ref[:, cols] = total[j, :, HALF:].astype(BF16)
 
     def sent(copy):
         def one(k, c):
@@ -280,16 +270,16 @@
         chunks = micro * per
         nb, nd = ff // HALF, pl.cdiv(ff, BLOCK)
         flat = (chunks, CHUNK, d)
-        reach, saved = OFF * (stages - 1), OFF * (stages - 2) + 1
+        reach, saved = OFF * (stages - 1), OFF * (stages - 2)
         grads = pl.pallas_call(
             functools.partial(kernel, stages, per, chunks),
             out_shape=[
-                jax.ShapeDtypeStruct((d, ff), BF16),
-                jax.ShapeDtypeStruct((d, ff), BF16),
-                jax.ShapeDtypeStruct((ff, d), BF16),
+                pltpu.VMEM((d, ff), BF16),
+                pltpu.VMEM((d, ff), BF16),
+                pltpu.VMEM((ff, d), BF16),
             ],
             in_specs=[pl.BlockSpec(memory_space=pl.ANY)] * 5,
-            out_specs=[pl.BlockSpec(memory_space=pl.ANY)] * 3,
+            out_specs=[pl.BlockSpec(memory_space=pltpu.VMEM)] * 3,
             scratch_shapes=[
                 pltpu.VMEM((reach + AHEAD, CHUNK, d), BF16),
                 pltpu.VMEM((reach + 1, CHUNK, d), BF16),
@@ -304,16 +294,14 @@
                 pltpu.VMEM((nb + nd, d, BLOCK), F32),
                 pltpu.VMEM((saved, CHUNK, ff), BF16),
                 pltpu.VMEM((saved, nb, CHUNK, BLOCK), F32),
-                pltpu.VMEM((CHUNK, nb * BLOCK), BF16),
                 pltpu.SemaphoreType.DMA((chunks,)),
                 pltpu.SemaphoreType.DMA((chunks,)),
                 pltpu.SemaphoreType.DMA((chunks,)),
                 pltpu.SemaphoreType.DMA((chunks,)),
                 pltpu.SemaphoreType.DMA((1 + 2 * nb,)),
-                pltpu.SemaphoreType.DMA((1 + 2 * nb,)),
             ],
             compiler_params=pltpu.CompilerParams(
-                collective_id=0, has_side_effects=True, vmem_limit_bytes=67_000_000
+                collective_id=0, has_side_effects=True, vmem_limit_bytes=61500000
             ),
         )(x.reshape(flat), dy.reshape(flat), w_gate[0], w_up[0], w_down[0])
         return tuple(g[None] for g in grads)

time: 154 us -> 143 us (0.929)
  Pallas kernels: 147 us -> 139 us
  local copies, waits for them, and re-layouts: 6.15 us -> 3.56 us
    pallas_call x1, Pallas kernels: 147 us -> 139 us  [step(): pl.pallas_call(functools.partial(kernel, stages, per, chunks), out_shape=...]
    unnamed x7 -> x3, local copies, waits for them, and re-layouts: 6.15 us -> 3.56 us
where the time goes in v2:
time: 143 us
  Pallas kernels  139 us (97%)
  local copies, waits for them, and re-layouts  3.56 us (2%)
    pallas_call x1, Pallas kernels, step(): pl.pallas_call(functools.partial(kernel, stages, per, chunks), out_shape=...  139 us
    unnamed x3, local copies, waits for them, and re-layouts  3.56 us

profile of v2, /device:TPU:112, one launch (start us, length us, event | category | flops | bytes accessed | tf_op | source)
XLA Modules:
  0.0 143.1 jit_solution(5320596028893394950)
XLA Ops:
  0.6 138.9 %shard_map.76 = (bf16[512,1664]{1,0:T(8,128)(2,1)S(1)}, bf16[512,1664]{1,0:T(8,128)(2,1)S(1)}, bf16[1664,512]{1,0:T(8,128)(2,1)S(1)}) custom-call(bf16[32,128,512]{2,1,0:T(8,128)(2,1)} %bitcast.11, bf16[32,128,512]{2,1,0:T(8,128)(2,1)} %bitcast.12, bf16[512,1664]{1,0:T(8,128)(2,1)} %bitcast.13, bf16[512,1664]{1,0:T(8,128)(2,1)} %bitcast.14, ...), custom_call_target="tpu_custom_call" | custom-call | tf_op jit(solution)/shard_map/pallas_call | solution.py:274
  139.5 1.2 copy.11
  140.7 1.2 copy.12
  141.9 1.2 copy.13

commit v3 on v2

--- a/solution.py
+++ b/solution.py
@@ -105,13 +105,14 @@
         scale = lax.rsqrt(jnp.mean(wide * wide, -1, keepdims=True) + EPS)
         return wide, scale, (wide * scale).astype(BF16)
 
+    def before_forward(k):
+        x_load(k).wait()
+
+        @pl.when(k >= OUT)
+        def _():
+            f_copy(k - OUT).wait_send()
+
     def forward(k):
-        x_load(k).wait()
-
-        @pl.when(k >= OUT)
-        def _():
-            f_copy(k - OUT).wait_send()
-
         slot = lax.rem(k, n_mid)
         wide, _, a = normed(kept[lax.rem(k, n_kept)])
         for j in range(nb):
@@ -126,68 +127,60 @@
         fout[lax.rem(k, OUT)] = (wide + y.astype(F32)).astype(BF16)
         f_copy(k).start()
 
-    def backward(k):
+    def before_backward(k):
+        @pl.when(last)
+        def _():
+            x_load(k).wait()
+
+        @pl.when(jnp.logical_not(first) & (k >= OUT))
+        def _():
+            b_copy(k - OUT).wait_send()
+
+        dy_load(k).wait()
+
+    def backward(k, again, onward):
         slot = lax.rem(lax.div(k, per), 2)
         mine = lax.rem(k, n_mid)
         here = lax.rem(k, n_kept)
         rows = pl.ds(pl.multiple_of(lax.rem(k, per) * CHUNK, CHUNK), CHUNK)
-
-        @pl.when(last)
-        def _():
-            x_load(k).wait()
-
-        @pl.when(jnp.logical_not(first) & (k >= OUT))
-        def _():
-            b_copy(k - OUT).wait_send()
-
-        dy_load(k).wait()
-
-        def chunk(again, onward):
-            by = byin[lax.rem(k, n_by)]
-            _, scale, a = normed(kept[here])
-            lhs[slot, 0, :, rows] = a.astype(F32).T.astype(BF16)
-            lhs[slot, 1, :, rows] = by.astype(F32).T.astype(BF16)
-            for jj in range(nd):
-                two = dot(by, wdt[jj]).astype(BF16).astype(F32)
-                for part in range(min(2, nb - 2 * jj)):
-                    j = 2 * jj + part
-                    dmid = two[:, part * HALF : (part + 1) * HALF]
-                    if again:
-                        gu = dot(a, wgu[j])
-                        g, u = gu[:, :HALF], gu[:, HALF:]
-                        s = sigmoid(g)
-                        silu = g * s
-                        slope, mid = u * (s + silu * (1.0 - s)), (silu * u).astype(BF16)
-                    else:
-                        slope, silu = slopes[mine, j, :, :HALF], slopes[mine, j, :, HALF:]
-                        mid = mids[mine, :, j * HALF : (j + 1) * HALF]
-                    dgate, dup = (dmid * slope).astype(BF16), (dmid * silu).astype(BF16)
-                    rhs[slot, nb + jj, rows, part * HALF : (part + 1) * HALF] = mid
-                    rhs[slot, j, rows, :HALF] = dgate
-                    rhs[slot, j, rows, HALF:] = dup
-            if onward:
-                da = dot(jnp.concatenate([rhs[slot, j, rows] for j in range(nb)], axis=1), wgut[...])
-                for lo in range(0, CHUNK, STRIP):
-                    part = slice(lo, lo + STRIP)
-                    wide, given = kept[here, part].astype(F32), byin[lax.rem(k, n_by), part].astype(F32)
-                    lead, each = scale[part], da[part].astype(BF16).astype(F32)
-                    lean = jnp.mean(each * wide, -1, keepdims=True) * lead * lead * lead
-                    dh = (each * lead - wide * lean).astype(BF16)
-                    bout[lax.rem(k, OUT), part] = (given + dh.astype(F32)).astype(BF16)
-                b_copy(k).start()
-
-        @pl.when(first)
-        def _():
-            chunk(True, False)
-
-        @pl.when(last)
-        def _():
-            chunk(True, True)
-
-        @pl.when(jnp.logical_not(first | last))
-        def _():
-            chunk(False, True)
-
+        by = byin[lax.rem(k, n_by)]
+        _, scale, a = normed(kept[here])
+        for jj in range(nd):
+            two = dot(by, wdt[jj]).astype(BF16).astype(F32)
+            for part in range(min(2, nb - 2 * jj)):
+                j = 2 * jj + part
+                dmid = two[:, part * HALF : (part + 1) * HALF]
+                if again:
+                    gu = dot(a, wgu[j])
+                    g, u = gu[:, :HALF], gu[:, HALF:]
+                    s = sigmoid(g)
+                    silu = g * s
+                    slope, mid = u * (s + silu * (1.0 - s)), (silu * u).astype(BF16)
+                else:
+                    slope, silu = slopes[mine, j, :, :HALF], slopes[mine, j, :, HALF:]
+                    mid = mids[mine, :, j * HALF : (j + 1) * HALF]
+                dgate, dup = (dmid * slope).astype(BF16), (dmid * silu).astype(BF16)
+                rhs[slot, nb + jj, rows, part * HALF : (part + 1) * HALF] = mid
+                rhs[slot, j, rows, :HALF] = dgate
+                rhs[slot, j, rows, HALF:] = dup
+        if onward:
+            da = dot(jnp.concatenate([rhs[slot, j, rows] for j in range(nb)], axis=1), wgut[...])
+            for lo in range(0, CHUNK, STRIP):
+                part = slice(lo, lo + STRIP)
+                wide, given = kept[here, part].astype(F32), byin[lax.rem(k, n_by), part].astype(F32)
+                lead, each = scale[part], da[part].astype(BF16).astype(F32)
+                lean = jnp.mean(each * wide, -1, keepdims=True) * lead * lead * lead
+                dh = (each * lead - wide * lean).astype(BF16)
+                bout[lax.rem(k, OUT), part] = (given + dh.astype(F32)).astype(BF16)
+            b_copy(k).start()
+
+    def turned(k):
+        slot = lax.rem(lax.div(k, per), 2)
+        rows = pl.ds(pl.multiple_of(lax.rem(k, per) * CHUNK, CHUNK), CHUNK)
+        lhs[slot, 0, :, rows] = normed(kept[lax.rem(k, n_kept)])[2].astype(F32).T.astype(BF16)
+        lhs[slot, 1, :, rows] = byin[lax.rem(k, n_by)].astype(F32).T.astype(BF16)
+
+    def after_backward(k):
         @pl.when(first & (k + n_kept < chunks))
         def _():
             x_load(k + n_kept).start()
@@ -212,37 +205,67 @@
             lo, hi = jj * BLOCK, min(ff, (jj + 1) * BLOCK)
             wdt[jj, :, : hi - lo] = wd[lo:hi, :].astype(F32).T.astype(BF16)
 
+    middle = jnp.logical_not(first | last)
+
     def step(i, carry):
         f, b = i, i - OFF * behind
         w = b - per
+        f_on = (f < chunks) & jnp.logical_not(last)
+        b_on = (b >= 0) & (b < chunks)
 
         @pl.when(i == jnp.where(first, 3, 0))
         def _():
             transposed()
 
-        @pl.when((b >= 0) & (b < chunks))
-        def _():
-            backward(b)
-
-        @pl.when((f < chunks) & jnp.logical_not(last))
-        def _():
+        @pl.when(b_on)
+        def _():
+            before_backward(b)
+
+        @pl.when(b_on & first)
+        def _():
+            backward(b, True, False)
+
+        @pl.when(b_on & middle)
+        def _():
+            backward(b, False, True)
+
+        @pl.when(b_on & last)
+        def _():
+            backward(b, True, True)
+
+        @pl.when(f_on)
+        def _():
+            before_forward(f)
             forward(f)
 
-        @pl.when((w >= 0) & (w < chunks))
+        @pl.when(b_on & (w >= 0))
         def _():
             products(w)
+            turned(b)
+
+        @pl.when(b_on & (w < 0))
+        def _():
+            turned(b)
+
+        @pl.when(b_on)
+        def _():
+            after_backward(b)
 
         return carry
 
-    lax.fori_loop(0, chunks + OFF * (stages - 1) + per, step, 0)
-
-    for jj in range(nd):
-        lo, hi = jj * BLOCK, min(ff, (jj + 1) * BLOCK)
-        od_ref[lo:hi, :] = total[nb + jj].T[: hi - lo].astype(BF16)
-    for j in range(nb):
-        cols = slice(j * HALF, (j + 1) * HALF)
-        og_ref[:, cols] = total[j, :, :HALF].astype(BF16)
-        ou_ref[:, cols] = total[j, :, HALF:].astype(BF16)
+    lax.fori_loop(0, chunks + OFF * (stages - 1), step, 0)
+
+    slot = (chunks // per - 1) % 2
+    for q in list(range(nb, nb + nd)) + list(range(nb)):
+        term = dot(lhs[slot, 1 if q >= nb else 0], rhs[slot, q]).astype(BF16)
+        done = total[q] + term.astype(F32)
+        if q >= nb:
+            lo, hi = (q - nb) * BLOCK, min(ff, (q - nb + 1) * BLOCK)
+            od_ref[lo:hi, :] = done.T[: hi - lo].astype(BF16)
+        else:
+            cols = slice(q * HALF, (q + 1) * HALF)
+            og_ref[:, cols] = done[:, :HALF].astype(BF16)
+            ou_ref[:, cols] = done[:, HALF:].astype(BF16)
 
     def sent(copy):
         def one(k, c):
@@ -258,6 +281,15 @@
     @pl.when(jnp.logical_not(first))
     def _():
         sent(b_copy)
+
+
+def put(*refs):
+    n = (len(refs) - 1) // 2
+    copies = [pltpu.make_async_copy(refs[i], refs[n + i], refs[-1].at[i]) for i in range(n)]
+    for copy in copies:
+        copy.start()
+    for copy in copies:
+        copy.wait()
 
 
 def solution(mesh):
@@ -304,6 +336,14 @@
                 collective_id=0, has_side_effects=True, vmem_limit_bytes=61500000
             ),
         )(x.reshape(flat), dy.reshape(flat), w_gate[0], w_up[0], w_down[0])
+        grads = pl.pallas_call(
+            put,
+            out_shape=[jax.ShapeDtypeStruct(g.shape, g.dtype) for g in grads],
+            in_specs=[pl.BlockSpec(memory_space=pl.ANY)] * 3,
+            out_specs=[pl.BlockSpec(memory_space=pl.ANY)] * 3,
+            scratch_shapes=[pltpu.SemaphoreType.DMA((3,))],
+            compiler_params=pltpu.CompilerParams(vmem_limit_bytes=1_000_000),
+        )(*grads)
         return tuple(g[None] for g in grads)
 
     return jax.shard_map(

time: 143 us -> 140 us (0.979)
  local copies, waits for them, and re-layouts: 3.56 us -> 0 us
    unnamed x3 -> x0, local copies, waits for them, and re-layouts: 3.56 us -> none
    pallas_call x0 -> x1, Pallas kernels: none -> 2.33 us  [step(): pl.pallas_call(put, out_shape=[jax.ShapeDtypeStruct(g.shape, g.dtype) for...]
    pallas_call x1, Pallas kernels: 139 us -> 137 us  [step(): pl.pallas_call(functools.partial(kernel, stages, per, chunks), out_shape=...]
where the time goes in v3:
time: 140 us
  Pallas kernels  140 us (100%)
    pallas_call x1, Pallas kernels, step(): pl.pallas_call(functools.partial(kernel, stages, per, chunks), out_shape=...  137 us

profile of v3, /device:TPU:112, one launch (start us, length us, event | category | flops | bytes accessed | tf_op | source)
XLA Modules:
  0.0 140.2 jit_solution(4504074152889204749)
XLA Ops:
  0.6 137.2 %shard_map.76 = (bf16[512,1664]{1,0:T(8,128)(2,1)S(1)}, bf16[512,1664]{1,0:T(8,128)(2,1)S(1)}, bf16[1664,512]{1,0:T(8,128)(2,1)S(1)}) custom-call(bf16[32,128,512]{2,1,0:T(8,128)(2,1)} %bitcast.8, bf16[32,128,512]{2,1,0:T(8,128)(2,1)} %bitcast.9, bf16[512,1664]{1,0:T(8,128)(2,1)} %bitcast.10, bf16[512,1664]{1,0:T(8,128)(2,1)} %bitcast.11, ...), custom_call_target="tpu_custom_call" | custom-call | tf_op jit(solution)/shard_map/pallas_call | solution.py:306
  137.8 2.3 %shard_map.77 = (bf16[512,1664]{1,0:T(8,128)(2,1)}, bf16[512,1664]{1,0:T(8,128)(2,1)}, bf16[1664,512]{1,0:T(8,128)(2,1)}) custom-call(bf16[512,1664]{1,0:T(8,128)(2,1)S(1)} %get-tuple-element.9.refs_0_, bf16[512,1664]{1,0:T(8,128)(2,1)S(1)} %get-tuple-element.10.refs_1_, bf16[1664,512]{1,0:T(8,128)(2,1)S(1)} %get-tuple-element.11.refs_2_), custom_call_target="tpu_custom_call" | custom-call | tf_op jit(solution)/shard_map/pallas_call | solution.py:339

commit v4 on v3

--- a/solution.py
+++ b/solution.py
@@ -10,7 +10,8 @@
 CHUNK = 128
 BLOCK = 256
 HALF = BLOCK // 2
-OFF = 5
+OFF = 4
+MORE = 1
 AHEAD = 5
 STRIP = 32
 OUT = 4
@@ -43,23 +44,33 @@
     nd = pl.cdiv(ff, BLOCK)
     quarter = (nb + nd) // per
 
-    loads = [pltpu.make_async_copy(wd_ref, wd, wsem.at[0])]
+    barrier = pltpu.get_barrier_semaphore()
+    for side in (left, right):
+        pl.semaphore_signal(barrier, inc=1, device_id={"pp": side}, device_id_type=MESH)
+
+    loads = []
     for j in range(nb):
         cols = pl.ds(j * HALF, HALF)
         loads.append(pltpu.make_async_copy(wg_ref.at[:, cols], wgu.at[j, :, pl.ds(0, HALF)], wsem.at[1 + 2 * j]))
         loads.append(pltpu.make_async_copy(wu_ref.at[:, cols], wgu.at[j, :, pl.ds(HALF, HALF)], wsem.at[2 + 2 * j]))
+    loads.append(pltpu.make_async_copy(wd_ref, wd, wsem.at[0]))
+
+    reach = OFF * (stages - 1) + MORE
+    n_kept, n_by, n_mid = kept.shape[0], byin.shape[0], mids.shape[0]
+    assert n_kept > reach + 1 and n_by > reach and n_mid > OFF * (stages - 2)
+
+    def x_load(k):
+        return pltpu.make_async_copy(x_ref.at[k], kept.at[lax.rem(k, n_kept)], frecv.at[k])
+
+    def dy_load(k):
+        return pltpu.make_async_copy(dy_ref.at[k], byin.at[lax.rem(k, n_by)], brecv.at[k])
+
+    @pl.when(first)
+    def _():
+        x_load(0).start()
+
     for load in loads:
         load.start()
-
-    reach = OFF * (stages - 1)
-    n_kept, n_by, n_mid = kept.shape[0], byin.shape[0], mids.shape[0]
-    assert n_kept > reach and n_by > reach and n_mid >= OFF * (stages - 2)
-
-    def x_load(k):
-        return pltpu.make_async_copy(x_ref.at[k], kept.at[lax.rem(k, n_kept)], frecv.at[k])
-
-    def dy_load(k):
-        return pltpu.make_async_copy(dy_ref.at[k], byin.at[lax.rem(k, n_by)], brecv.at[k])
 
     @pl.when(first)
     def _():
@@ -67,7 +78,7 @@
             x_load(k).start()
             return c
 
-        lax.fori_loop(0, min(chunks, n_kept), go, 0)
+        lax.fori_loop(1, min(chunks, n_kept), go, 0)
 
     @pl.when(last)
     def _():
@@ -76,10 +87,6 @@
             return c
 
         lax.fori_loop(0, min(chunks, n_by), go, 0)
-
-    barrier = pltpu.get_barrier_semaphore()
-    for side in (left, right):
-        pl.semaphore_signal(barrier, inc=1, device_id={"pp": side}, device_id_type=MESH)
 
     total[...] = jnp.zeros_like(total)
     rhs[:, nb + nd - 1] = jnp.zeros_like(rhs[:, nb + nd - 1])
@@ -208,7 +215,7 @@
     middle = jnp.logical_not(first | last)
 
     def step(i, carry):
-        f, b = i, i - OFF * behind
+        f, b = i, i - OFF * behind - jnp.where(first, MORE, 0)
         w = b - per
         f_on = (f < chunks) & jnp.logical_not(last)
         b_on = (b >= 0) & (b < chunks)
@@ -217,27 +224,27 @@
         def _():
             transposed()
 
-        @pl.when(b_on)
-        def _():
-            before_backward(b)
-
-        @pl.when(b_on & first)
-        def _():
-            backward(b, True, False)
-
-        @pl.when(b_on & middle)
-        def _():
-            backward(b, False, True)
-
-        @pl.when(b_on & last)
-        def _():
-            backward(b, True, True)
-
         @pl.when(f_on)
         def _():
             before_forward(f)
             forward(f)
 
+        @pl.when(b_on)
+        def _():
+            before_backward(b)
+
+        @pl.when(b_on & first)
+        def _():
+            backward(b, True, False)
+
+        @pl.when(b_on & middle)
+        def _():
+            backward(b, False, True)
+
+        @pl.when(b_on & last)
+        def _():
+            backward(b, True, True)
+
         @pl.when(b_on & (w >= 0))
         def _():
             products(w)
@@ -253,7 +260,7 @@
 
         return carry
 
-    lax.fori_loop(0, chunks + OFF * (stages - 1), step, 0)
+    lax.fori_loop(0, chunks + reach, step, 0)
 
     slot = (chunks // per - 1) % 2
     for q in list(range(nb, nb + nd)) + list(range(nb)):
@@ -302,7 +309,7 @@
         chunks = micro * per
         nb, nd = ff // HALF, pl.cdiv(ff, BLOCK)
         flat = (chunks, CHUNK, d)
-        reach, saved = OFF * (stages - 1), OFF * (stages - 2)
+        reach, saved = OFF * (stages - 1) + MORE, OFF * (stages - 2) + 1
         grads = pl.pallas_call(
             functools.partial(kernel, stages, per, chunks),
             out_shape=[

time: 140 us -> 137 us (0.979)
  Pallas kernels: 140 us -> 137 us
    pallas_call x1, Pallas kernels: 137 us -> 134 us  [step(): pl.pallas_call(functools.partial(kernel, stages, per, chunks), out_shape=...]
where the time goes in v4:
time: 137 us
  Pallas kernels  137 us (100%)
    pallas_call x1, Pallas kernels, step(): pl.pallas_call(functools.partial(kernel, stages, per, chunks), out_shape=...  134 us

profile of v4, /device:TPU:112, one launch (start us, length us, event | category | flops | bytes accessed | tf_op | source)
XLA Modules:
  0.0 137.2 jit_solution(12375517162298474589)
XLA Ops:
  0.6 134.2 %shard_map.76 = (bf16[512,1664]{1,0:T(8,128)(2,1)S(1)}, bf16[512,1664]{1,0:T(8,128)(2,1)S(1)}, bf16[1664,512]{1,0:T(8,128)(2,1)S(1)}) custom-call(bf16[32,128,512]{2,1,0:T(8,128)(2,1)} %bitcast.8, bf16[32,128,512]{2,1,0:T(8,128)(2,1)} %bitcast.9, bf16[512,1664]{1,0:T(8,128)(2,1)} %bitcast.10, bf16[512,1664]{1,0:T(8,128)(2,1)} %bitcast.11, ...), custom_call_target="tpu_custom_call" | custom-call | tf_op jit(solution)/shard_map/pallas_call | solution.py:313
  134.9 2.3 %shard_map.77 = (bf16[512,1664]{1,0:T(8,128)(2,1)}, bf16[512,1664]{1,0:T(8,128)(2,1)}, bf16[1664,512]{1,0:T(8,128)(2,1)}) custom-call(bf16[512,1664]{1,0:T(8,128)(2,1)S(1)} %get-tuple-element.9.refs_0_, bf16[512,1664]{1,0:T(8,128)(2,1)S(1)} %get-tuple-element.10.refs_1_, bf16[1664,512]{1,0:T(8,128)(2,1)S(1)} %get-tuple-element.11.refs_2_), custom_call_target="tpu_custom_call" | custom-call | tf_op jit(solution)/shard_map/pallas_call | solution.py:346

commit v5 on v4

--- a/solution.py
+++ b/solution.py
@@ -14,6 +14,7 @@
 MORE = 1
 AHEAD = 5
 STRIP = 32
+SHIP = 4
 OUT = 4
 EPS = 1e-6
 F32, BF16 = jnp.float32, jnp.bfloat16
@@ -31,8 +32,8 @@
 def kernel(
     stages, per, chunks,
     x_ref, dy_ref, wg_ref, wu_ref, wd_ref,
-    og_ref, ou_ref, od_ref,
-    kept, byin, fout, bout, wgu, wgut, wd, wdt, rhs, lhs, total, mids, slopes,
+    total, lhs, rhs,
+    kept, byin, fout, bout, wgu, wgut, wd, wdt, mids, slopes,
     fsend, frecv, bsend, brecv, wsem,
 ):
     me = lax.axis_index("pp")
@@ -262,39 +263,48 @@
 
     lax.fori_loop(0, chunks + reach, step, 0)
 
-    slot = (chunks // per - 1) % 2
-    for q in list(range(nb, nb + nd)) + list(range(nb)):
+    def sent(copy):
+        def one(k, c):
+            copy(k).wait_send()
+            return c
+
+        lax.fori_loop(max(0, chunks - OUT), chunks, one, 0)
+
+    @pl.when(jnp.logical_not(last))
+    def _():
+        sent(f_copy)
+
+    @pl.when(jnp.logical_not(first))
+    def _():
+        sent(b_copy)
+
+
+def finish(slot, nb, total, lhs, rhs, og_ref, ou_ref, od_ref, og, ou, od, sem):
+    ff = od.shape[0]
+    nd = total.shape[0] - nb
+    copies = []
+
+    def leave(source, target):
+        copies.append(pltpu.make_async_copy(source, target, sem.at[len(copies)]))
+        copies[-1].start()
+
+    for q in [*range(nb, nb + nd), *range(nb)]:
         term = dot(lhs[slot, 1 if q >= nb else 0], rhs[slot, q]).astype(BF16)
         done = total[q] + term.astype(F32)
         if q >= nb:
             lo, hi = (q - nb) * BLOCK, min(ff, (q - nb + 1) * BLOCK)
-            od_ref[lo:hi, :] = done.T[: hi - lo].astype(BF16)
+            od[lo:hi, :] = done.T[: hi - lo].astype(BF16)
+            if q == nb + nd - 1:
+                leave(od, od_ref)
         else:
             cols = slice(q * HALF, (q + 1) * HALF)
-            og_ref[:, cols] = done[:, :HALF].astype(BF16)
-            ou_ref[:, cols] = done[:, HALF:].astype(BF16)
-
-    def sent(copy):
-        def one(k, c):
-            copy(k).wait_send()
-            return c
-
-        lax.fori_loop(max(0, chunks - OUT), chunks, one, 0)
-
-    @pl.when(jnp.logical_not(last))
-    def _():
-        sent(f_copy)
-
-    @pl.when(jnp.logical_not(first))
-    def _():
-        sent(b_copy)
-
-
-def put(*refs):
-    n = (len(refs) - 1) // 2
-    copies = [pltpu.make_async_copy(refs[i], refs[n + i], refs[-1].at[i]) for i in range(n)]
-    for copy in copies:
-        copy.start()
+            og[:, cols] = done[:, :HALF].astype(BF16)
+            ou[:, cols] = done[:, HALF:].astype(BF16)
+            if q % SHIP == SHIP - 1 or q == nb - 1:
+                lo = q // SHIP * SHIP * HALF
+                cols = pl.ds(lo, (q + 1) * HALF - lo)
+                leave(og.at[:, cols], og_ref.at[:, cols])
+                leave(ou.at[:, cols], ou_ref.at[:, cols])
     for copy in copies:
         copy.wait()
 
@@ -310,12 +320,12 @@
         nb, nd = ff // HALF, pl.cdiv(ff, BLOCK)
         flat = (chunks, CHUNK, d)
         reach, saved = OFF * (stages - 1) + MORE, OFF * (stages - 2) + 1
-        grads = pl.pallas_call(
+        sums = pl.pallas_call(
             functools.partial(kernel, stages, per, chunks),
             out_shape=[
-                pltpu.VMEM((d, ff), BF16),
-                pltpu.VMEM((d, ff), BF16),
-                pltpu.VMEM((ff, d), BF16),
+                pltpu.VMEM((nb + nd, d, BLOCK), F32),
+                pltpu.VMEM((2, 2, d, tokens), BF16),
+                pltpu.VMEM((2, nb + nd, tokens, BLOCK), BF16),
             ],
             in_specs=[pl.BlockSpec(memory_space=pl.ANY)] * 5,
             out_specs=[pl.BlockSpec(memory_space=pltpu.VMEM)] * 3,
@@ -328,9 +338,6 @@
                 pltpu.VMEM((nb * BLOCK, d), BF16),
                 pltpu.VMEM((ff, d), BF16),
                 pltpu.VMEM((nd, d, BLOCK), BF16),
-                pltpu.VMEM((2, nb + nd, tokens, BLOCK), BF16),
-                pltpu.VMEM((2, 2, d, tokens), BF16),
-                pltpu.VMEM((nb + nd, d, BLOCK), F32),
                 pltpu.VMEM((saved, CHUNK, ff), BF16),
                 pltpu.VMEM((saved, nb, CHUNK, BLOCK), F32),
                 pltpu.SemaphoreType.DMA((chunks,)),
@@ -340,17 +347,18 @@
                 pltpu.SemaphoreType.DMA((1 + 2 * nb,)),
             ],
             compiler_params=pltpu.CompilerParams(
-                collective_id=0, has_side_effects=True, vmem_limit_bytes=61500000
+                collective_id=0, has_side_effects=True, vmem_limit_bytes=43_000_000
             ),
         )(x.reshape(flat), dy.reshape(flat), w_gate[0], w_up[0], w_down[0])
+        shapes = [(d, ff), (d, ff), (ff, d)]
         grads = pl.pallas_call(
-            put,
-            out_shape=[jax.ShapeDtypeStruct(g.shape, g.dtype) for g in grads],
-            in_specs=[pl.BlockSpec(memory_space=pl.ANY)] * 3,
+            functools.partial(finish, (micro - 1) % 2, nb),
+            out_shape=[jax.ShapeDtypeStruct(shape, BF16) for shape in shapes],
+            in_specs=[pl.BlockSpec(memory_space=pltpu.VMEM)] * 3,
             out_specs=[pl.BlockSpec(memory_space=pl.ANY)] * 3,
-            scratch_shapes=[pltpu.SemaphoreType.DMA((3,))],
-            compiler_params=pltpu.CompilerParams(vmem_limit_bytes=1_000_000),
-        )(*grads)
+            scratch_shapes=[*(pltpu.VMEM(shape, BF16) for shape in shapes), pltpu.SemaphoreType.DMA((2 * nb + 1,))],
+            compiler_params=pltpu.CompilerParams(vmem_limit_bytes=16_000_000),
+        )(*sums)
         return tuple(g[None] for g in grads)
 
     return jax.shard_map(

time: 137 us -> 137 us (level)
    pallas_call x1, Pallas kernels: 134 us -> 132 us  [step(): pl.pallas_call(functools.partial(kernel, stages, per, chunks), out_shape=...]
    pallas_call x1, Pallas kernels: 2.33 us -> 4.36 us  [step(): pl.pallas_call(functools.partial(finish, (micro - 1) % 2, nb), out_shape=...]
where the time goes in v5:
time: 137 us
  Pallas kernels  136 us (99%)
    pallas_call x1, Pallas kernels, step(): pl.pallas_call(functools.partial(kernel, stages, per, chunks), out_shape=...  132 us
    pallas_call x1, Pallas kernels, step(): pl.pallas_call(functools.partial(finish, (micro - 1) % 2, nb), out_shape=...  4.36 us

profile of v5, /device:TPU:112, one launch (start us, length us, event | category | flops | bytes accessed | tf_op | source)
XLA Modules:
  0.0 136.7 jit_solution(5854848142480662774)
XLA Ops:
  0.6 131.7 %shard_map.76 = (f32[20,512,256]{2,1,0:T(8,128)S(1)}, bf16[2,2,512,512]{3,2,1,0:T(8,128)(2,1)S(1)}, bf16[2,20,512,256]{3,2,1,0:T(8,128)(2,1)S(1)}) custom-call(bf16[32,128,512]{2,1,0:T(8,128)(2,1)} %bitcast.8, bf16[32,128,512]{2,1,0:T(8,128)(2,1)} %bitcast.9, bf16[512,1664]{1,0:T(8,128)(2,1)} %bitcast.10, bf16[512,1664]{1,0:T(8,128)(2,1)} %bitcast.11, ...), custom_call_target="tpu_custom_call" | custom-call | tf_op jit(solution)/shard_map/pallas_call | solution.py:323
  132.4 4.4 %shard_map.77 = (bf16[512,1664]{1,0:T(8,128)(2,1)}, bf16[512,1664]{1,0:T(8,128)(2,1)}, bf16[1664,512]{1,0:T(8,128)(2,1)}) custom-call(f32[20,512,256]{2,1,0:T(8,128)S(1)} %get-tuple-element.9.total, bf16[2,2,512,512]{3,2,1,0:T(8,128)(2,1)S(1)} %get-tuple-element.10.lhs, bf16[2,20,512,256]{3,2,1,0:T(8,128)(2,1)S(1)} %get-tuple-element.11.rhs), custom_call_target="tpu_custom_call" | custom-call | tf_op jit(solution)/shard_map/pallas_call | solution.py:354

commit v6 on v5

--- a/solution.py
+++ b/solution.py
@@ -58,7 +58,7 @@
 
     reach = OFF * (stages - 1) + MORE
     n_kept, n_by, n_mid = kept.shape[0], byin.shape[0], mids.shape[0]
-    assert n_kept > reach + 1 and n_by > reach and n_mid > OFF * (stages - 2)
+    assert n_kept > reach + 1 and n_by > reach and n_mid > OFF * (stages - 2) and n_mid <= reach
 
     def x_load(k):
         return pltpu.make_async_copy(x_ref.at[k], kept.at[lax.rem(k, n_kept)], frecv.at[k])
@@ -230,14 +230,26 @@
             before_forward(f)
             forward(f)
 
+        ending = b >= chunks - per
+
+        @pl.when(b_on & ending)
+        def _():
+            products(w)
+
         @pl.when(b_on)
         def _():
             before_backward(b)
 
-        @pl.when(b_on & first)
+        held = b >= chunks - n_mid
+
+        @pl.when(b_on & first & jnp.logical_not(held))
         def _():
             backward(b, True, False)
 
+        @pl.when(b_on & first & held)
+        def _():
+            backward(b, False, False)
+
         @pl.when(b_on & middle)
         def _():
             backward(b, False, True)
@@ -246,12 +258,12 @@
         def _():
             backward(b, True, True)
 
-        @pl.when(b_on & (w >= 0))
+        @pl.when(b_on & (w >= 0) & jnp.logical_not(ending))
         def _():
             products(w)
             turned(b)
 
-        @pl.when(b_on & (w < 0))
+        @pl.when(b_on & ((w < 0) | ending))
         def _():
             turned(b)
 

time: 137 us -> 135 us (0.985)
  no operation moved by 1% of the time
where the time goes in v6:
time: 135 us
  Pallas kernels  135 us (100%)
    pallas_call x1, Pallas kernels, step(): pl.pallas_call(functools.partial(kernel, stages, per, chunks), out_shape=...  130 us
    pallas_call x1, Pallas kernels, step(): pl.pallas_call(functools.partial(finish, (micro - 1) % 2, nb), out_shape=...  4.36 us

profile of v6, /device:TPU:112, one launch (start us, length us, event | category | flops | bytes accessed | tf_op | source)
XLA Modules:
  0.0 135.4 jit_solution(10376525759645628159)
XLA Ops:
  0.6 130.4 %shard_map.76 = (f32[20,512,256]{2,1,0:T(8,128)S(1)}, bf16[2,2,512,512]{3,2,1,0:T(8,128)(2,1)S(1)}, bf16[2,20,512,256]{3,2,1,0:T(8,128)(2,1)S(1)}) custom-call(bf16[32,128,512]{2,1,0:T(8,128)(2,1)} %bitcast.8, bf16[32,128,512]{2,1,0:T(8,128)(2,1)} %bitcast.9, bf16[512,1664]{1,0:T(8,128)(2,1)} %bitcast.10, bf16[512,1664]{1,0:T(8,128)(2,1)} %bitcast.11, ...), custom_call_target="tpu_custom_call" | custom-call | tf_op jit(solution)/shard_map/pallas_call | solution.py:335
  131.0 4.4 %shard_map.77 = (bf16[512,1664]{1,0:T(8,128)(2,1)}, bf16[512,1664]{1,0:T(8,128)(2,1)}, bf16[1664,512]{1,0:T(8,128)(2,1)}) custom-call(f32[20,512,256]{2,1,0:T(8,128)S(1)} %get-tuple-element.9.total, bf16[2,2,512,512]{3,2,1,0:T(8,128)(2,1)S(1)} %get-tuple-element.10.lhs, bf16[2,20,512,256]{3,2,1,0:T(8,128)(2,1)S(1)} %get-tuple-element.11.rhs), custom_call_target="tpu_custom_call" | custom-call | tf_op jit(solution)/shard_map/pallas_call | solution.py:366
